TPU v7x, 32 devices: a whole 2x2x4 slice. The times are simulated.
32 devices in a mesh: src: 8 (over z, core), tgt: 4 (over y, x).
Axes of the slice: x: 2, y: 2, z: 4, core: 2. Of those that a mesh axis runs over, the one named last changes fastest.
Arguments:
- source_embed: bfloat16 [128, 128, 128], P('src', None, 'tgt'), may hold values from -4 to 4
- target_embed: bfloat16 [64, 128, 128], P('tgt', None, 'src'), may hold values from -4 to 4
- source_mass: float32 [128, 128], P('src'), may hold values from 10 to 14
- target_mass: float32 [64, 128], P('tgt'), may hold values from 10 to 14
- target_start: float32 [64, 128], P('tgt'), may hold values from -6 to 6
- block_pairs: int32 [8, 4, 128, 2], P('src', 'tgt'), may hold values from 0 to 15, as said below
- counts: int32 [8, 4], P('src', 'tgt'), may hold values from 16 to 128, as said below
Outputs:
- sender_log_scaling: float32 [128, 128], P('src')
- target_dual_potential: float32 [64, 128], P('tgt')
Inputs may be any that keep to these rules, and one draw needn't show every extreme that they name: `block_pairs`: entry 0 of a slot is a local source block (below 16), entry 1 a local target block (below 16). The live slots of a device name distinct pairs; its first 16 slots name each of its target blocks once and each of its source blocks at least once. Slots at or past the device's count are not kept and hold arbitrary block numbers. `counts`: some device has all 128 slots live in every draw.
All inputs are finite; a program needn't handle non-finite values.
Results may differ from a plain program's by a relative error of at most 0.0003.
Values may be sent and summed in bfloat16 or wider, within the bound.
A program may use at most 64 MiB of HBM per device.

v0:
```python
import functools
import math

import jax
import jax.numpy as jnp
from jax import lax
from jax.experimental import pallas as pl
from jax.experimental.pallas import tpu as pltpu
from jax.sharding import PartitionSpec as P

ITERS = 2

smoothing_epsilon = 4.0
dead_score = -1e30
log2_e = math.log2(math.e)
ln_2 = math.log(2.0)
column_group = 4
feature_tile = 16


def merge(parts):
    peak = functools.reduce(jnp.maximum, parts)
    total = functools.reduce(jnp.add, [jnp.exp2(part - peak) for part in parts])
    return peak + jnp.log2(total)


def kernel(
    n_src,
    n_tgt,
    gather_here,
    source_ref,
    target_ref,
    source_mass_ref,
    target_mass_ref,
    start_ref,
    plan_ref,
    count_ref,
    source_out,
    target_out,
    score,
    source_full,
    target_full,
    spread,
    bias,
    potential,
    row_parts,
    col_parts,
    own_sems,
    gs_send,
    gs_recv,
    gt_send,
    gt_recv,
    row_send,
    row_recv,
    col_send,
    col_recv,
):
    s, t = lax.axis_index("src"), lax.axis_index("tgt")
    source_blocks, target_blocks, frames, _ = score.shape
    sizes = {"src": n_src, "tgt": n_tgt}
    here = {"src": s, "tgt": t}

    def peer(axis, step):
        return lax.rem(here[axis] + step, sizes[axis])

    barrier = pltpu.get_barrier_semaphore()
    for axis in ("src", "tgt"):
        for step in range(1, sizes[axis]):
            pl.semaphore_signal(
                barrier,
                inc=1,
                device_id={axis: peer(axis, step)},
                device_id_type=pl.DeviceIdType.MESH,
            )
    pl.semaphore_wait(barrier, n_src + n_tgt - 2)

    def remote(src, dst, send, recv, axis, step):
        return pltpu.make_async_remote_copy(
            src_ref=src,
            dst_ref=dst,
            send_sem=send,
            recv_sem=recv,
            device_id={axis: peer(axis, step)},
            device_id_type=pl.DeviceIdType.MESH,
        )

    def gather_copies(local, full, send, recv, axis):
        width = local.shape[1]

        def slot(owner):
            return full.at[:, pl.ds(pl.multiple_of(owner * width, width), width), :]

        out, arrive = [], []
        for step in range(1, sizes[axis]):
            out.append(
                remote(local, slot(here[axis]), send.at[step], recv.at[step], axis, step)
            )
            sender = lax.rem(here[axis] + sizes[axis] - step, sizes[axis])
            arrive.append(
                remote(local, slot(sender), send.at[step], recv.at[step], axis, step)
            )
        return out, arrive, slot(here[axis])

    if gather_here:
        s_out, s_in, s_own = gather_copies(source_ref, source_full, gs_send, gs_recv, "tgt")
        t_out, t_in, t_own = gather_copies(target_ref, target_full, gt_send, gt_recv, "src")
        for copy in t_out + s_out:
            copy.start()
        own = [
            pltpu.make_async_copy(source_ref, s_own, own_sems.at[0]),
            pltpu.make_async_copy(target_ref, t_own, own_sems.at[1]),
        ]
    else:
        own = [
            pltpu.make_async_copy(source_ref, source_full, own_sems.at[0]),
            pltpu.make_async_copy(target_ref, target_full, own_sems.at[1]),
        ]
    for copy in own:
        copy.start()

    slots = plan_ref.shape[1]
    live = lax.broadcasted_iota(jnp.int32, (source_blocks, slots), 1) < count_ref[0, 0]
    near = lax.broadcasted_iota(jnp.int32, (source_blocks, slots), 0) == plan_ref[0:1, :]
    far = lax.broadcasted_iota(jnp.int32, (target_blocks, slots), 0) == plan_ref[1:2, :]
    near = jnp.where(near & live, 1.0, 0.0).astype(jnp.bfloat16)
    far = jnp.where(far, 1.0, 0.0).astype(jnp.bfloat16)
    kept = lax.dot_general(
        near, far, (((1,), (1,)), ((), ())), preferred_element_type=jnp.float32
    )
    for block in range(target_blocks):
        bias[block] = jnp.broadcast_to(
            jnp.where(kept[:, block : block + 1] > 0.5, 0.0, dead_score),
            (source_blocks, frames),
        )
    potential[...] = start_ref[...] * log2_e

    diagonal = lax.broadcasted_iota(jnp.int32, (frames, frames), 0) == (
        lax.broadcasted_iota(jnp.int32, (frames, frames), 1)
    )

    for copy in own:
        copy.wait()
    if gather_here:
        for copy in s_in + t_in:
            copy.wait_recv()

    def row_block(block, parts, make_scores):
        if make_scores:
            left = source_full[block].T
        peak = None
        for other in range(0, target_blocks, 2):
            if make_scores:
                right = jnp.concatenate(
                    [target_full[other], target_full[other + 1]], axis=1
                )
                product = jnp.dot(left, right, preferred_element_type=jnp.float32)
            for k in range(2):
                if make_scores:
                    tile = product[:, k * frames : (k + 1) * frames] * (
                        log2_e / smoothing_epsilon
                    ) + bias[other + k, pl.ds(block, 1), :]
                    score[block, other + k] = tile
                else:
                    tile = score[block, other + k]
                tile = tile + potential[other + k : other + k + 1, :]
                peak = tile if peak is None else jnp.maximum(peak, tile)
        peak = jnp.max(peak, axis=1, keepdims=True)
        total = None
        for other in range(target_blocks):
            term = jnp.exp2(
                score[block, other] + potential[other : other + 1, :] - peak
            )
            total = term if total is None else total + term
        total = jnp.sum(total, axis=1, keepdims=True)
        column = peak + jnp.log2(total)
        row = jnp.sum(jnp.where(diagonal, column, 0.0), axis=0, keepdims=True)
        parts[0, pl.ds(block, 1), :] = row

    def column_group_stats(first, parts):
        start = jnp.full((8, frames), 2 * dead_score, jnp.float32)

        def fold(value):
            return value.reshape(frames // 8, 8, frames)

        def tile(block, k):
            return score[block, first + k] + spread[block]

        def peaks(block, current):
            return tuple(
                jnp.maximum(current[k], jnp.max(fold(tile(block, k)), axis=0))
                for k in range(column_group)
            )

        peak = lax.fori_loop(0, source_blocks, peaks, (start,) * column_group)
        peak = [jnp.max(p, axis=0, keepdims=True) for p in peak]

        def sums(block, current):
            return tuple(
                current[k] + jnp.sum(fold(jnp.exp2(tile(block, k) - peak[k])), axis=0)
                for k in range(column_group)
            )

        total = lax.fori_loop(
            0, source_blocks, sums, (jnp.zeros((8, frames), jnp.float32),) * column_group
        )
        for k in range(column_group):
            parts[0, pl.ds(first + k, 1), :] = peak[k] + jnp.log2(
                jnp.sum(total[k], axis=0, keepdims=True)
            )

    sends = []

    def exchange(parts, send, recv, axis):
        copies = [
            remote(parts.at[0], parts.at[step], send.at[step], recv.at[step], axis, step)
            for step in range(1, sizes[axis])
        ]
        for copy in copies:
            copy.start()
        for copy in copies:
            copy.wait_recv()
        sends.extend(copies)
        return merge([parts[step] for step in range(sizes[axis])])

    for iteration in range(ITERS):
        parts = row_parts.at[iteration]

        def rows(block, carry):
            row_block(block, parts, iteration == 0)
            return carry

        lax.fori_loop(0, source_blocks, rows, 0)
        sender = source_mass_ref[...] * log2_e - exchange(
            parts, row_send.at[iteration], row_recv.at[iteration], "tgt"
        )
        if iteration == ITERS - 1:
            source_out[...] = sender * ln_2
        for block in range(source_blocks):
            column = jnp.sum(
                jnp.where(diagonal, sender[block : block + 1, :], 0.0),
                axis=1,
                keepdims=True,
            )
            spread[block] = jnp.broadcast_to(column, (frames, frames))
        parts = col_parts.at[iteration]

        def columns(group, carry):
            column_group_stats(group * column_group, parts)
            return carry

        lax.fori_loop(0, target_blocks // column_group, columns, 0)
        dual = target_mass_ref[...] * log2_e - exchange(
            parts, col_send.at[iteration], col_recv.at[iteration], "src"
        )
        if iteration == ITERS - 1:
            target_out[...] = dual * ln_2
        else:
            potential[...] = dual

    if gather_here:
        sends.extend(s_out + t_out)
    for copy in sends:
        copy.wait_send()


def on_device(
    n_src,
    n_tgt,
    source_embed,
    target_embed,
    source_mass,
    target_mass,
    target_start,
    block_pairs,
    counts,
):
    source = jnp.swapaxes(source_embed, 1, 2)
    target = jnp.swapaxes(target_embed, 1, 2)
    source_blocks, source_width, frames = source.shape
    target_blocks, target_width, _ = target.shape
    gather_here = source_width % feature_tile == 0 and target_width % feature_tile == 0
    if not gather_here:
        source = lax.all_gather(source, "tgt", axis=1, tiled=True)
        target = lax.all_gather(target, "src", axis=1, tiled=True)
    features = source_width * n_tgt
    plan = block_pairs.reshape(block_pairs.shape[2], 2).T
    dma = pltpu.SemaphoreType.DMA
    vmem = pl.BlockSpec(memory_space=pltpu.VMEM)
    return pl.pallas_call(
        functools.partial(kernel, n_src, n_tgt, gather_here),
        out_shape=(
            jax.ShapeDtypeStruct(source_mass.shape, jnp.float32),
            jax.ShapeDtypeStruct(target_mass.shape, jnp.float32),
        ),
        in_specs=[vmem] * 6 + [pl.BlockSpec(memory_space=pltpu.SMEM)],
        out_specs=(vmem, vmem),
        scratch_shapes=[
            pltpu.VMEM((source_blocks, target_blocks, frames, frames), jnp.float32),
            pltpu.VMEM((source_blocks, features, frames), jnp.bfloat16),
            pltpu.VMEM((target_blocks, features, frames), jnp.bfloat16),
            pltpu.VMEM((source_blocks, frames, frames), jnp.float32),
            pltpu.VMEM((target_blocks, source_blocks, frames), jnp.float32),
            pltpu.VMEM((target_blocks, frames), jnp.float32),
            pltpu.VMEM((ITERS, n_tgt, source_blocks, frames), jnp.float32),
            pltpu.VMEM((ITERS, n_src, target_blocks, frames), jnp.float32),
            dma((2,)),
            dma((n_tgt,)),
            dma((n_tgt,)),
            dma((n_src,)),
            dma((n_src,)),
            dma((ITERS, n_tgt)),
            dma((ITERS, n_tgt)),
            dma((ITERS, n_src)),
            dma((ITERS, n_src)),
        ],
        compiler_params=pltpu.CompilerParams(
            collective_id=0, has_side_effects=True, vmem_limit_bytes=40 * 2**20
        ),
        name="sinkhorn",
    )(source, target, source_mass, target_mass, target_start, plan, counts)


def solution(mesh):
    in_specs = (
        P("src", None, "tgt"),
        P("tgt", None, "src"),
        P("src", None),
        P("tgt", None),
        P("tgt", None),
        P("src", "tgt", None, None),
        P("src", "tgt"),
    )
    out_specs = (P("src", None), P("tgt", None))
    return jax.shard_map(
        functools.partial(on_device, mesh.shape["src"], mesh.shape["tgt"]),
        mesh=mesh,
        in_specs=in_specs,
        out_specs=out_specs,
        check_vma=False,
    )
```

profile of v0, /device:TPU:0, one launch (start us, length us, event | category | flops | bytes accessed | tf_op | source)
XLA Modules:
  0.0 64.8 jit_solution(16670920612777210225)
XLA Ops:
  1.3 0.0 copy-start.5
  1.3 0.7 %copy-done.5 = s32[1,1,128,2]{2,3,1,0:T(2,128)S(1)} copy-done((s32[1,1,128,2]{2,3,1,0:T(2,128)S(1)}, s32[1,1,128,2]{2,3,1,0:T(2,128)}, u32[]{:S(2)}) %copy-start.5) | copy-done | bytes 1048
  2.0 0.0 copy-start
  2.0 0.9 %copy-done = bf16[16,128,32]{1,2,0:T(8,128)(2,1)S(1)} copy-done((bf16[16,128,32]{1,2,0:T(8,128)(2,1)S(1)}, bf16[16,128,32]{1,2,0:T(8,128)(2,1)}, u32[]{:S(2)}) %copy-start) | copy-done | bytes 131096
  2.9 0.0 copy-start.1
  2.9 0.8 %copy-done.1 = bf16[16,128,16]{1,2,0:T(8,128)(2,1)S(1)} copy-done((bf16[16,128,16]{1,2,0:T(8,128)(2,1)S(1)}, bf16[16,128,16]{1,2,0:T(8,128)(2,1)}, u32[]{:S(2)}) %copy-start.1) | copy-done | bytes 65560
  3.7 0.0 copy-start.2
  3.7 0.7 %copy-done.2 = f32[16,128]{1,0:T(8,128)S(1)} copy-done((f32[16,128]{1,0:T(8,128)S(1)}, f32[16,128]{1,0:T(8,128)}, u32[]{:S(2)}) %copy-start.2) | copy-done | bytes 8216
  4.4 0.0 copy-start.3
  4.4 0.7 %copy-done.3 = f32[16,128]{1,0:T(8,128)S(1)} copy-done((f32[16,128]{1,0:T(8,128)S(1)}, f32[16,128]{1,0:T(8,128)}, u32[]{:S(2)}) %copy-start.3) | copy-done | bytes 8216
  5.1 0.0 copy-start.4
  5.1 0.7 %copy-done.4 = f32[16,128]{1,0:T(8,128)S(1)} copy-done((f32[16,128]{1,0:T(8,128)S(1)}, f32[16,128]{1,0:T(8,128)}, u32[]{:S(2)}) %copy-start.4) | copy-done | bytes 8216
  5.8 57.8 %sinkhorn.1 = (f32[16,128]{1,0:T(8,128)S(1)}, f32[16,128]{1,0:T(8,128)S(1)}) custom-call(bf16[16,32,128]{2,1,0:T(8,128)(2,1)S(1)} %bitcast.5, bf16[16,16,128]{2,1,0:T(8,128)(2,1)S(1)} %bitcast.6, f32[16,128]{1,0:T(8,128)S(1)} %copy-done.2, f32[16,128]{1,0:T(8,128)S(1)} %copy-done.3, f32[16,128]{1,0:T(8,128)S(1)} %copy-done.4, s32[2,128]{1,0:T(2,128)S(1)} %bitcast.7, ...), custom_call_target="tpu_custom_call" | custom-call | tf_op jit(solution)/shard_map/sinkhorn/pallas_call | solution.py:289
  63.6 0.6 copy.12
  64.2 0.6 copy.13
Async XLA Ops:
  1.3 0.7 %copy-start.5 = (s32[1,1,128,2]{2,3,1,0:T(2,128)S(1)}, s32[1,1,128,2]{2,3,1,0:T(2,128)}, u32[]{:S(2)}) copy-start(s32[1,1,128,2]{2,3,1,0:T(2,128)} %param.12) | copy-start | bytes 3076
  2.0 0.9 %copy-start = (bf16[16,128,32]{1,2,0:T(8,128)(2,1)S(1)}, bf16[16,128,32]{1,2,0:T(8,128)(2,1)}, u32[]{:S(2)}) copy-start(bf16[16,128,32]{1,2,0:T(8,128)(2,1)} %param.7) | copy-start | bytes 393220
  2.9 0.8 %copy-start.1 = (bf16[16,128,16]{1,2,0:T(8,128)(2,1)S(1)}, bf16[16,128,16]{1,2,0:T(8,128)(2,1)}, u32[]{:S(2)}) copy-start(bf16[16,128,16]{1,2,0:T(8,128)(2,1)} %param.8) | copy-start | bytes 196612
  3.7 0.7 %copy-start.2 = (f32[16,128]{1,0:T(8,128)S(1)}, f32[16,128]{1,0:T(8,128)}, u32[]{:S(2)}) copy-start(f32[16,128]{1,0:T(8,128)} %source_mass_ref.1) | copy-start | bytes 24580
  4.4 0.7 %copy-start.3 = (f32[16,128]{1,0:T(8,128)S(1)}, f32[16,128]{1,0:T(8,128)}, u32[]{:S(2)}) copy-start(f32[16,128]{1,0:T(8,128)} %target_mass_ref.1) | copy-start | bytes 24580
  5.1 0.7 %copy-start.4 = (f32[16,128]{1,0:T(8,128)S(1)}, f32[16,128]{1,0:T(8,128)}, u32[]{:S(2)}) copy-start(f32[16,128]{1,0:T(8,128)} %start_ref.1) | copy-start | bytes 24580
where the time goes:
time: 65.2 us; the launch traced here: 64.8 us
  Pallas kernels  57.8 us (89%)
  local copies, waits for them, and re-layouts  5.7 us (9%)
  between operations  1.3 us (2%)
    pallas_call x1, Pallas kernels, on_device(): pl.pallas_call(functools.partial(kernel, n_src, n_tgt, gather_here), out_...  57.8 us
    unnamed x14, local copies, waits for them, and re-layouts  5.7 us

commit v1 on v0

--- a/solution.py
+++ b/solution.py
@@ -103,9 +103,33 @@
 
     if gather_here:
         s_out, s_in, s_own = gather_copies(source_ref, source_full, gs_send, gs_recv, "tgt")
-        t_out, t_in, t_own = gather_copies(target_ref, target_full, gt_send, gt_recv, "src")
+        width = target_ref.shape[1]
+        partner = s + 1 - 2 * lax.rem(s, 2)
+
+        def target_slot(owner):
+            return target_full.at[:, pl.ds(pl.multiple_of(owner * width, width), width), :]
+
+        def target_copy(src, owner, index, device):
+            return pltpu.make_async_remote_copy(
+                src_ref=src,
+                dst_ref=target_slot(owner),
+                send_sem=gt_send.at[index],
+                recv_sem=gt_recv.at[index],
+                device_id={"src": device},
+                device_id_type=pl.DeviceIdType.MESH,
+            )
+
+        t_own = target_slot(s)
+        t_out = [
+            target_copy(target_ref, s, step, peer("src", step))
+            for step in range(2, n_src, 2)
+        ]
         for copy in t_out + s_out:
             copy.start()
+        across = target_copy(target_ref, s, 1, partner)
+        across.start()
+        t_out.append(across)
+        t_in = [target_copy(target_ref, partner, 1, partner)]
         own = [
             pltpu.make_async_copy(source_ref, s_own, own_sems.at[0]),
             pltpu.make_async_copy(target_ref, t_own, own_sems.at[1]),
@@ -132,7 +156,9 @@
             jnp.where(kept[:, block : block + 1] > 0.5, 0.0, dead_score),
             (source_blocks, frames),
         )
-    potential[...] = start_ref[...] * log2_e
+    dual = start_ref[...] * log2_e
+    sender = None
+    potential[...] = dual
 
     diagonal = lax.broadcasted_iota(jnp.int32, (frames, frames), 0) == (
         lax.broadcasted_iota(jnp.int32, (frames, frames), 1)
@@ -141,6 +167,14 @@
     for copy in own:
         copy.wait()
     if gather_here:
+        for step in range(2, n_src, 2):
+            owner = lax.rem(s + n_src - step, n_src)
+            target_copy(target_ref, owner, step, owner).wait_recv()
+            relay = target_copy(target_slot(owner), owner, step + 1, partner)
+            relay.start()
+            t_out.append(relay)
+            owner = lax.rem(partner + n_src - step, n_src)
+            t_in.append(target_copy(target_ref, owner, step + 1, partner))
         for copy in s_in + t_in:
             copy.wait_recv()
 
@@ -159,17 +193,15 @@
                     tile = product[:, k * frames : (k + 1) * frames] * (
                         log2_e / smoothing_epsilon
                     ) + bias[other + k, pl.ds(block, 1), :]
-                    score[block, other + k] = tile
                 else:
                     tile = score[block, other + k]
                 tile = tile + potential[other + k : other + k + 1, :]
+                score[block, other + k] = tile
                 peak = tile if peak is None else jnp.maximum(peak, tile)
         peak = jnp.max(peak, axis=1, keepdims=True)
         total = None
         for other in range(target_blocks):
-            term = jnp.exp2(
-                score[block, other] + potential[other : other + 1, :] - peak
-            )
+            term = jnp.exp2(score[block, other] - peak)
             total = term if total is None else total + term
         total = jnp.sum(total, axis=1, keepdims=True)
         column = peak + jnp.log2(total)
@@ -182,21 +214,21 @@
         def fold(value):
             return value.reshape(frames // 8, 8, frames)
 
-        def tile(block, k):
-            return score[block, first + k] + spread[block]
-
         def peaks(block, current):
-            return tuple(
-                jnp.maximum(current[k], jnp.max(fold(tile(block, k)), axis=0))
-                for k in range(column_group)
-            )
+            raised = []
+            for k in range(column_group):
+                tile = score[block, first + k] + spread[block]
+                score[block, first + k] = tile
+                raised.append(jnp.maximum(current[k], jnp.max(fold(tile), axis=0)))
+            return tuple(raised)
 
         peak = lax.fori_loop(0, source_blocks, peaks, (start,) * column_group)
         peak = [jnp.max(p, axis=0, keepdims=True) for p in peak]
 
         def sums(block, current):
             return tuple(
-                current[k] + jnp.sum(fold(jnp.exp2(tile(block, k) - peak[k])), axis=0)
+                current[k]
+                + jnp.sum(fold(jnp.exp2(score[block, first + k] - peak[k])), axis=0)
                 for k in range(column_group)
             )
 
@@ -230,14 +262,18 @@
             return carry
 
         lax.fori_loop(0, source_blocks, rows, 0)
-        sender = source_mass_ref[...] * log2_e - exchange(
+        fresh = source_mass_ref[...] * log2_e - exchange(
             parts, row_send.at[iteration], row_recv.at[iteration], "tgt"
         )
+        if sender is None:
+            shift = sender = fresh
+        else:
+            shift, sender = fresh, fresh + sender
         if iteration == ITERS - 1:
             source_out[...] = sender * ln_2
         for block in range(source_blocks):
             column = jnp.sum(
-                jnp.where(diagonal, sender[block : block + 1, :], 0.0),
+                jnp.where(diagonal, shift[block : block + 1, :], 0.0),
                 axis=1,
                 keepdims=True,
             )
@@ -249,13 +285,14 @@
             return carry
 
         lax.fori_loop(0, target_blocks // column_group, columns, 0)
-        dual = target_mass_ref[...] * log2_e - exchange(
+        fresh = target_mass_ref[...] * log2_e - exchange(
             parts, col_send.at[iteration], col_recv.at[iteration], "src"
         )
+        dual = fresh + dual
         if iteration == ITERS - 1:
             target_out[...] = dual * ln_2
         else:
-            potential[...] = dual
+            potential[...] = fresh
 
     if gather_here:
         sends.extend(s_out + t_out)

time: 65.2 us -> 61.9 us (0.949)
  Pallas kernels: 57.8 us -> 54.5 us
    pallas_call x1, Pallas kernels: 57.8 us -> 54.5 us  [on_device(): pl.pallas_call(functools.partial(kernel, n_src, n_tgt, gather_here), out_...]
where the time goes in v1:
time: 61.9 us; the launch traced here: 61.5 us
  Pallas kernels  54.5 us (88%)
  local copies, waits for them, and re-layouts  5.7 us (9%)
  between operations  1.3 us (2%)
    pallas_call x1, Pallas kernels, on_device(): pl.pallas_call(functools.partial(kernel, n_src, n_tgt, gather_here), out_...  54.5 us
    unnamed x14, local copies, waits for them, and re-layouts  5.7 us

profile of v1, /device:TPU:0, one launch (start us, length us, event | category | flops | bytes accessed | tf_op | source)
XLA Modules:
  0.0 61.5 jit_solution(893730327498627396)
XLA Ops:
  1.3 0.0 copy-start.5
  1.3 0.7 %copy-done.5 = s32[1,1,128,2]{2,3,1,0:T(2,128)S(1)} copy-done((s32[1,1,128,2]{2,3,1,0:T(2,128)S(1)}, s32[1,1,128,2]{2,3,1,0:T(2,128)}, u32[]{:S(2)}) %copy-start.5) | copy-done | bytes 1048
  2.0 0.0 copy-start
  2.0 0.9 %copy-done = bf16[16,128,32]{1,2,0:T(8,128)(2,1)S(1)} copy-done((bf16[16,128,32]{1,2,0:T(8,128)(2,1)S(1)}, bf16[16,128,32]{1,2,0:T(8,128)(2,1)}, u32[]{:S(2)}) %copy-start) | copy-done | bytes 131096
  2.9 0.0 copy-start.1
  2.9 0.8 %copy-done.1 = bf16[16,128,16]{1,2,0:T(8,128)(2,1)S(1)} copy-done((bf16[16,128,16]{1,2,0:T(8,128)(2,1)S(1)}, bf16[16,128,16]{1,2,0:T(8,128)(2,1)}, u32[]{:S(2)}) %copy-start.1) | copy-done | bytes 65560
  3.7 0.0 copy-start.2
  3.7 0.7 %copy-done.2 = f32[16,128]{1,0:T(8,128)S(1)} copy-done((f32[16,128]{1,0:T(8,128)S(1)}, f32[16,128]{1,0:T(8,128)}, u32[]{:S(2)}) %copy-start.2) | copy-done | bytes 8216
  4.4 0.0 copy-start.3
  4.4 0.7 %copy-done.3 = f32[16,128]{1,0:T(8,128)S(1)} copy-done((f32[16,128]{1,0:T(8,128)S(1)}, f32[16,128]{1,0:T(8,128)}, u32[]{:S(2)}) %copy-start.3) | copy-done | bytes 8216
  5.1 0.0 copy-start.4
  5.1 0.7 %copy-done.4 = f32[16,128]{1,0:T(8,128)S(1)} copy-done((f32[16,128]{1,0:T(8,128)S(1)}, f32[16,128]{1,0:T(8,128)}, u32[]{:S(2)}) %copy-start.4) | copy-done | bytes 8216
  5.8 54.5 %sinkhorn.1 = (f32[16,128]{1,0:T(8,128)S(1)}, f32[16,128]{1,0:T(8,128)S(1)}) custom-call(bf16[16,32,128]{2,1,0:T(8,128)(2,1)S(1)} %bitcast.5, bf16[16,16,128]{2,1,0:T(8,128)(2,1)S(1)} %bitcast.6, f32[16,128]{1,0:T(8,128)S(1)} %copy-done.2, f32[16,128]{1,0:T(8,128)S(1)} %copy-done.3, f32[16,128]{1,0:T(8,128)S(1)} %copy-done.4, s32[2,128]{1,0:T(2,128)S(1)} %bitcast.7, ...), custom_call_target="tpu_custom_call" | custom-call | tf_op jit(solution)/shard_map/sinkhorn/pallas_call | solution.py:326
  60.3 0.6 copy.12
  60.9 0.6 copy.13
Async XLA Ops:
  1.3 0.7 %copy-start.5 = (s32[1,1,128,2]{2,3,1,0:T(2,128)S(1)}, s32[1,1,128,2]{2,3,1,0:T(2,128)}, u32[]{:S(2)}) copy-start(s32[1,1,128,2]{2,3,1,0:T(2,128)} %param.12) | copy-start | bytes 3076
  2.0 0.9 %copy-start = (bf16[16,128,32]{1,2,0:T(8,128)(2,1)S(1)}, bf16[16,128,32]{1,2,0:T(8,128)(2,1)}, u32[]{:S(2)}) copy-start(bf16[16,128,32]{1,2,0:T(8,128)(2,1)} %param.7) | copy-start | bytes 393220
  2.9 0.8 %copy-start.1 = (bf16[16,128,16]{1,2,0:T(8,128)(2,1)S(1)}, bf16[16,128,16]{1,2,0:T(8,128)(2,1)}, u32[]{:S(2)}) copy-start(bf16[16,128,16]{1,2,0:T(8,128)(2,1)} %param.8) | copy-start | bytes 196612
  3.7 0.7 %copy-start.2 = (f32[16,128]{1,0:T(8,128)S(1)}, f32[16,128]{1,0:T(8,128)}, u32[]{:S(2)}) copy-start(f32[16,128]{1,0:T(8,128)} %source_mass_ref.1) | copy-start | bytes 24580
  4.4 0.7 %copy-start.3 = (f32[16,128]{1,0:T(8,128)S(1)}, f32[16,128]{1,0:T(8,128)}, u32[]{:S(2)}) copy-start(f32[16,128]{1,0:T(8,128)} %target_mass_ref.1) | copy-start | bytes 24580
  5.1 0.7 %copy-start.4 = (f32[16,128]{1,0:T(8,128)S(1)}, f32[16,128]{1,0:T(8,128)}, u32[]{:S(2)}) copy-start(f32[16,128]{1,0:T(8,128)} %start_ref.1) | copy-start | bytes 24580

commit v2 on v1

--- a/solution.py
+++ b/solution.py
@@ -222,7 +222,7 @@
                 raised.append(jnp.maximum(current[k], jnp.max(fold(tile), axis=0)))
             return tuple(raised)
 
-        peak = lax.fori_loop(0, source_blocks, peaks, (start,) * column_group)
+        peak = lax.fori_loop(0, source_blocks, peaks, (start,) * column_group, unroll=4)
         peak = [jnp.max(p, axis=0, keepdims=True) for p in peak]
 
         def sums(block, current):
@@ -233,7 +233,8 @@
             )
 
         total = lax.fori_loop(
-            0, source_blocks, sums, (jnp.zeros((8, frames), jnp.float32),) * column_group
+            0, source_blocks, sums, (jnp.zeros((8, frames), jnp.float32),) * column_group,
+            unroll=4,
         )
         for k in range(column_group):
             parts[0, pl.ds(first + k, 1), :] = peak[k] + jnp.log2(
@@ -261,7 +262,7 @@
             row_block(block, parts, iteration == 0)
             return carry
 
-        lax.fori_loop(0, source_blocks, rows, 0)
+        lax.fori_loop(0, source_blocks, rows, 0, unroll=2)
         fresh = source_mass_ref[...] * log2_e - exchange(
             parts, row_send.at[iteration], row_recv.at[iteration], "tgt"
         )

time: 61.9 us -> 56.1 us (0.906)
  Pallas kernels: 54.5 us -> 48.7 us
    pallas_call x1, Pallas kernels: 54.5 us -> 48.7 us  [on_device(): pl.pallas_call(functools.partial(kernel, n_src, n_tgt, gather_here), out_...]
where the time goes in v2:
time: 56.1 us; the launch traced here: 55.7 us
  Pallas kernels  48.7 us (87%)
  local copies, waits for them, and re-layouts  5.7 us (10%)
  between operations  1.3 us (2%)
    pallas_call x1, Pallas kernels, on_device(): pl.pallas_call(functools.partial(kernel, n_src, n_tgt, gather_here), out_...  48.7 us
    unnamed x14, local copies, waits for them, and re-layouts  5.7 us

profile of v2, /device:TPU:0, one launch (start us, length us, event | category | flops | bytes accessed | tf_op | source)
XLA Modules:
  0.0 55.7 jit_solution(1618686246307945318)
XLA Ops:
  1.3 0.0 copy-start.5
  1.3 0.7 %copy-done.5 = s32[1,1,128,2]{2,3,1,0:T(2,128)S(1)} copy-done((s32[1,1,128,2]{2,3,1,0:T(2,128)S(1)}, s32[1,1,128,2]{2,3,1,0:T(2,128)}, u32[]{:S(2)}) %copy-start.5) | copy-done | bytes 1048
  2.0 0.0 copy-start
  2.0 0.9 %copy-done = bf16[16,128,32]{1,2,0:T(8,128)(2,1)S(1)} copy-done((bf16[16,128,32]{1,2,0:T(8,128)(2,1)S(1)}, bf16[16,128,32]{1,2,0:T(8,128)(2,1)}, u32[]{:S(2)}) %copy-start) | copy-done | bytes 131096
  2.9 0.0 copy-start.1
  2.9 0.8 %copy-done.1 = bf16[16,128,16]{1,2,0:T(8,128)(2,1)S(1)} copy-done((bf16[16,128,16]{1,2,0:T(8,128)(2,1)S(1)}, bf16[16,128,16]{1,2,0:T(8,128)(2,1)}, u32[]{:S(2)}) %copy-start.1) | copy-done | bytes 65560
  3.7 0.0 copy-start.2
  3.7 0.7 %copy-done.2 = f32[16,128]{1,0:T(8,128)S(1)} copy-done((f32[16,128]{1,0:T(8,128)S(1)}, f32[16,128]{1,0:T(8,128)}, u32[]{:S(2)}) %copy-start.2) | copy-done | bytes 8216
  4.4 0.0 copy-start.3
  4.4 0.7 %copy-done.3 = f32[16,128]{1,0:T(8,128)S(1)} copy-done((f32[16,128]{1,0:T(8,128)S(1)}, f32[16,128]{1,0:T(8,128)}, u32[]{:S(2)}) %copy-start.3) | copy-done | bytes 8216
  5.1 0.0 copy-start.4
  5.1 0.7 %copy-done.4 = f32[16,128]{1,0:T(8,128)S(1)} copy-done((f32[16,128]{1,0:T(8,128)S(1)}, f32[16,128]{1,0:T(8,128)}, u32[]{:S(2)}) %copy-start.4) | copy-done | bytes 8216
  5.8 48.7 %sinkhorn.1 = (f32[16,128]{1,0:T(8,128)S(1)}, f32[16,128]{1,0:T(8,128)S(1)}) custom-call(bf16[16,32,128]{2,1,0:T(8,128)(2,1)S(1)} %bitcast.5, bf16[16,16,128]{2,1,0:T(8,128)(2,1)S(1)} %bitcast.6, f32[16,128]{1,0:T(8,128)S(1)} %copy-done.2, f32[16,128]{1,0:T(8,128)S(1)} %copy-done.3, f32[16,128]{1,0:T(8,128)S(1)} %copy-done.4, s32[2,128]{1,0:T(2,128)S(1)} %bitcast.7, ...), custom_call_target="tpu_custom_call" | custom-call | tf_op jit(solution)/shard_map/sinkhorn/pallas_call | solution.py:327
  54.5 0.6 %copy.12 = f32[16,128]{1,0:T(8,128)} copy(f32[16,128]{1,0:T(8,128)S(1)} %get-tuple-element.4) | data formatting | bytes 16384
  55.1 0.6 %copy.13 = f32[16,128]{1,0:T(8,128)} copy(f32[16,128]{1,0:T(8,128)S(1)} %get-tuple-element.5) | data formatting | bytes 16384
Async XLA Ops:
  1.3 0.7 %copy-start.5 = (s32[1,1,128,2]{2,3,1,0:T(2,128)S(1)}, s32[1,1,128,2]{2,3,1,0:T(2,128)}, u32[]{:S(2)}) copy-start(s32[1,1,128,2]{2,3,1,0:T(2,128)} %param.12) | copy-start | bytes 3076
  2.0 0.9 %copy-start = (bf16[16,128,32]{1,2,0:T(8,128)(2,1)S(1)}, bf16[16,128,32]{1,2,0:T(8,128)(2,1)}, u32[]{:S(2)}) copy-start(bf16[16,128,32]{1,2,0:T(8,128)(2,1)} %param.7) | copy-start | bytes 393220
  2.9 0.8 %copy-start.1 = (bf16[16,128,16]{1,2,0:T(8,128)(2,1)S(1)}, bf16[16,128,16]{1,2,0:T(8,128)(2,1)}, u32[]{:S(2)}) copy-start(bf16[16,128,16]{1,2,0:T(8,128)(2,1)} %param.8) | copy-start | bytes 196612
  3.7 0.7 %copy-start.2 = (f32[16,128]{1,0:T(8,128)S(1)}, f32[16,128]{1,0:T(8,128)}, u32[]{:S(2)}) copy-start(f32[16,128]{1,0:T(8,128)} %source_mass_ref.1) | copy-start | bytes 24580
  4.4 0.7 %copy-start.3 = (f32[16,128]{1,0:T(8,128)S(1)}, f32[16,128]{1,0:T(8,128)}, u32[]{:S(2)}) copy-start(f32[16,128]{1,0:T(8,128)} %target_mass_ref.1) | copy-start | bytes 24580
  5.1 0.7 %copy-start.4 = (f32[16,128]{1,0:T(8,128)S(1)}, f32[16,128]{1,0:T(8,128)}, u32[]{:S(2)}) copy-start(f32[16,128]{1,0:T(8,128)} %start_ref.1) | copy-start | bytes 24580
